TPU v7x, 512 devices: a whole 4x8x8 slice. The times are simulated.
512 devices in a mesh: seq: 64 (over z, x, core), width: 8 (over y).
Axes of the slice: x: 4, y: 8, z: 8, core: 2. Of those that a mesh axis runs over, the one named last changes fastest.
Arguments:
- fade_rate: float32 [2, 32768, 2048], P(None, 'seq', 'width'), may hold values from 0.2 to 2
- update_in: bfloat16 [2, 32768, 2048], P(None, 'seq', 'width'), may hold values from -6 to 6
- gate_in: bfloat16 [2, 32768, 2048], P(None, 'seq', 'width'), may hold values from -6 to 6
Outputs:
- filtered: bfloat16 [2, 32768, 2048], P(None, 'seq', 'width')
All inputs are finite; a program needn't handle non-finite values.
Results may differ from a plain program's by a relative error of at most 0.0015.
Values sent between devices are 32-bit elements; how exact they have to be, the bound alone decides.
A program may use at most 64 MiB of HBM per device.

v0:
```python
import jax
import jax.numpy as jnp
from jax import lax
from jax.sharding import Mesh
from jax.sharding import PartitionSpec as P

SEQ = ("seq_0", "seq_1", "seq_2")


def filled_with(value, identity):
    return jax.tree.map(
        lambda a, e: jnp.broadcast_to(jnp.asarray(e, a.dtype), a.shape), value, identity
    )


def collected_together(value, axis):
    leaves = jax.tree.leaves(value)
    sequence = sorted(range(len(leaves)), key=lambda k: -leaves[k].size)
    width = (1, *leaves[sequence[0]].shape)[-1]
    lines = [
        jnp.pad(leaves[k].reshape(-1), (0, -leaves[k].size % width)).reshape(-1, width)
        for k in sequence
    ]
    both, at, found = (lax.all_gather(jnp.concatenate(lines), axis), 0, {})
    for k, line in zip(sequence, lines):
        share = both[:, at : at + len(line)].reshape(len(both), -1)
        found[k] = share[:, : leaves[k].size].reshape(-1, *leaves[k].shape)
        at += len(line)
    numbers = iter(range(len(leaves)))
    return jax.tree.map(lambda _: found[next(numbers)], value)


def carried_in(value, axes, combine, identity, reverse):
    before = start = filled_with(value, identity)
    running = value
    for axis in reversed(axes):
        peers, index = (lax.axis_size(axis), lax.axis_index(axis))
        pieces = collected_together(running, axis)
        inside, running = (start, start)
        for k in reversed(range(peers)) if reverse else range(peers):
            passed = k > index if reverse else k < index
            running = combine(running, jax.tree.map(lambda part: part[k], pieces))
            inside = jax.tree.map(lambda new, old: jnp.where(passed, new, old), running, inside)
        before = combine(inside, before)
    return before


def join_pair(earlier, later):
    return (earlier[0] * later[0], later[0] * earlier[1] + later[1])


def local(fade_rate, update_in, gate_in):
    total_length = fade_rate.shape[1] * lax.axis_size(SEQ)
    keep = jnp.exp(-fade_rate / total_length)
    push = update_in.astype(jnp.float32) * total_length ** (-0.5)
    steps = -fade_rate / total_length
    logs = jnp.sum(steps, axis=1, keepdims=True) - jnp.cumsum(steps, axis=1)
    later_logs = logs
    summary = (jnp.exp(jnp.sum(steps, axis=1)), jnp.sum(jnp.exp(later_logs) * push, axis=1))
    entering_forward = carried_in(
        summary, SEQ, join_pair, (jnp.ones_like(keep[:, 0]), jnp.zeros_like(push[:, 0])), False
    )
    started = push.at[:, 0].add(keep[:, 0] * entering_forward[1])
    forward = lax.associative_scan(join_pair, (keep, started), axis=1)[1]
    steps = -fade_rate / total_length
    logs = jnp.cumsum(steps, axis=1)
    before_logs = logs - steps
    summary = (jnp.exp(logs[:, -1]), jnp.sum(jnp.exp(before_logs) * push, axis=1))
    entering_backward = carried_in(
        summary, SEQ, join_pair, (jnp.ones_like(keep[:, 0]), jnp.zeros_like(push[:, 0])), True
    )
    started = push.at[:, -1].add(keep[:, -1] * entering_backward[1])
    backward = lax.associative_scan(join_pair, (keep, started), axis=1, reverse=True)[1]
    states = forward + backward
    gated = states * jax.nn.silu(gate_in.astype(jnp.float32))
    filtered = gated.astype(jnp.bfloat16)
    return filtered


def solution(mesh):
    split = Mesh(
        mesh.devices.reshape(8, 4, 2, mesh.shape["width"]), ("seq_0", "seq_1", "seq_2", "width")
    )
    in_specs = (P(None, SEQ, "width"), P(None, SEQ, "width"), P(None, SEQ, "width"))
    out_specs = P(None, SEQ, "width")
    return jax.shard_map(local, mesh=split, in_specs=in_specs, out_specs=out_specs, check_vma=False)
```

profile of v0, /device:TPU:8, one launch (start us, length us, event | category | flops | bytes accessed | tf_op | source)
XLA Modules:
  0.0 144.0 jit_solution(4338814983236438491)
XLA Ops:
  0.0 1.4 fusion.58
  1.4 0.7 fusion.4
  2.2 0.2 broadcast_add_fusion
  2.3 0.2 copy.53
  2.6 0.7 slice.757
  3.3 0.7 slice.753
  4.0 2.6 %slice.857 = f32[2,256,256]{2,1,0:T(8,128)} reverse(f32[2,256,256]{2,1,0:T(8,128)S(1)} %slice.753), dimensions={1} | reverse | bytes 1048576 | tf_op jit(solution)/shard_map/slice | solution.py:73
  6.6 2.6 %slice.851 = f32[2,256,256]{2,1,0:T(8,128)} reverse(f32[2,256,256]{2,1,0:T(8,128)S(1)} %slice.757), dimensions={1} | reverse | bytes 1048576 | tf_op jit(solution)/shard_map/slice | solution.py:73
  9.1 2.2 %slice.849 = f32[2,255,256]{2,1,0:T(8,128)} slice(f32[2,512,256]{2,1,0:T(8,128)S(1)} %get-tuple-element.35), slice={[0:2:1], [1:510:2], [0:256:1]} | slice | bytes 1044480 | tf_op jit(solution)/shard_map/slice | solution.py:73
  11.3 4.9 %slice.850 = f32[2,255,256]{2,1,0:T(8,128)} reverse(f32[2,255,256]{2,1,0:T(8,128)} %slice.849), dimensions={1} | reverse | bytes 1044480 | tf_op jit(solution)/shard_map/slice | solution.py:73
  16.2 2.2 %slice.752 = f32[2,255,256]{2,1,0:T(8,128)} slice(f32[2,512,256]{2,1,0:T(8,128)S(1)} %get-tuple-element.35), slice={[0:2:1], [2:512:2], [0:256:1]} | slice | bytes 1044480 | tf_op jit(solution)/shard_map/slice | solution.py:64
  18.3 2.2 %multiply_reduce_fusion.1 = (f32[2,256]{1,0:T(2,128)S(1)}, f32[2,256]{1,0:T(2,128)S(1)}, f32[2,512,256]{2,1,0:T(8,128)S(1)}) fusion(f32[2,256]{1,0:T(2,128)S(1)} %get-tuple-element.36, bf16[2,512,256]{2,1,0:T(8,128)(2,1)} %param.8, f32[2,256,4,128]{1,3,2,0:T(8,128)} %copy-done, f32[2,512,256]{2,1,0:T(8,128)} %param.7), kind=kLoop, calls=%fused_computation.9 | loop fusion | flops 2620416 | bytes 3676160 | tf_op jit(solution)/shard_map/reduce_sum | solution.py:59
  20.5 1.8 %all-gather.9 = f32[2,4,256]{2,1,0:T(4,128)S(1)} all-gather(f32[1,4,256]{2,1,0:T(4,128)S(1)} %maximum_bitcast_fusion.3), channel_id=5, replica_groups=mesh['seq_0'=8,'seq_1'=4,'seq_2'=2,'width'=8] {'seq_2'}, dimensions={0}, use_global_device_ids=true | all-gather | bytes 12288 | tf_op jit(solution)/shard_map/all_gather | solution.py:24
  22.4 1.8 %all-gather.6 = f32[2,4,256]{2,1,0:T(4,128)S(1)} all-gather(f32[1,4,256]{2,1,0:T(4,128)S(1)} %maximum_bitcast_fusion), channel_id=2, replica_groups=mesh['seq_0'=8,'seq_1'=4,'seq_2'=2,'width'=8] {'seq_2'}, dimensions={0}, use_global_device_ids=true | all-gather | bytes 12288 | tf_op jit(solution)/shard_map/all_gather | solution.py:24
  24.2 12.4 %all-gather.10 = f32[4,4,256]{2,1,0:T(4,128)S(1)} all-gather(f32[1,4,256]{2,1,0:T(4,128)S(1)} %maximum_bitcast_fusion.4), channel_id=6, replica_groups=mesh['seq_0'=8,'seq_1'=4,'seq_2'=2,'width'=8] {'seq_1'}, dimensions={0}, use_global_device_ids=true | all-gather | bytes 20480 | tf_op jit(solution)/shard_map/all_gather | solution.py:24
  36.7 12.0 %all-gather.7 = f32[4,4,256]{2,1,0:T(4,128)S(1)} all-gather(f32[1,4,256]{2,1,0:T(4,128)S(1)} %maximum_bitcast_fusion.1), channel_id=3, replica_groups=mesh['seq_0'=8,'seq_1'=4,'seq_2'=2,'width'=8] {'seq_1'}, dimensions={0}, use_global_device_ids=true | all-gather | bytes 20480 | tf_op jit(solution)/shard_map/all_gather | solution.py:24
  48.8 31.0 %all-gather.8 = f32[8,4,256]{2,1,0:T(4,128)S(1)} all-gather(f32[1,4,256]{2,1,0:T(4,128)S(1)} %maximum_bitcast_fusion.2), channel_id=4, replica_groups=mesh['seq_0'=8,'seq_1'=4,'seq_2'=2,'width'=8] {'seq_0'}, dimensions={0}, use_global_device_ids=true | all-gather | bytes 36864 | tf_op jit(solution)/shard_map/all_gather | solution.py:24
  79.8 0.1 slice_add_fusion.5
  79.9 24.7 %all-gather.11 = f32[8,4,256]{2,1,0:T(4,128)S(1)} all-gather(f32[1,4,256]{2,1,0:T(4,128)S(1)} %maximum_bitcast_fusion.5), channel_id=7, replica_groups=mesh['seq_0'=8,'seq_1'=4,'seq_2'=2,'width'=8] {'seq_0'}, dimensions={0}, use_global_device_ids=true | all-gather | bytes 36864 | tf_op jit(solution)/shard_map/all_gather | solution.py:24
  104.6 0.1 copy.457
  104.8 2.2 %slice.817 = f32[2,255,256]{2,1,0:T(8,128)} slice(f32[2,512,256]{2,1,0:T(8,128)S(1)} %scatter-add.6), slice={[0:2:1], [2:512:2], [0:256:1]} | slice | bytes 1044480 | tf_op jit(solution)/shard_map/slice | solution.py:64
  107.0 2.2 %slice.755 = f32[2,256,256]{2,1,0:T(8,128)} slice(f32[2,512,256]{2,1,0:T(8,128)S(1)} %scatter-add.6), slice={[0:2:1], [1:512:2], [0:256:1]} | slice | bytes 1048576 | tf_op jit(solution)/shard_map/slice | solution.py:64
  109.2 2.1 %slice.754 = f32[2,256,256]{2,1,0:T(8,128)} slice(f32[2,512,256]{2,1,0:T(8,128)S(1)} %scatter-add.6), slice={[0:2:1], [0:511:2], [0:256:1]} | slice | bytes 1048576 | tf_op jit(solution)/shard_map/slice | solution.py:64
  111.3 1.3 fusion.59
  112.7 0.1 slice.763
  112.8 0.1 slice.759
  113.0 0.2 slice.758
  113.2 0.2 slice.815
  113.4 0.1 slice.761
  113.6 0.1 slice.760
  113.7 0.1 fusion.61
  115.8 0.1 fusion.10
  116.0 0.1 pad.128
  116.1 0.1 pad.129
  116.2 0.8 copy-done.5
  117.0 0.2 copy-done.4
  117.2 0.1 fusion.8
  117.3 0.1 add.584
  117.5 2.1 %pad.130 = f32[2,512,256]{2,1,0:T(8,128)} pad(f32[2,256,256]{2,1,0:T(8,128)S(1)} %pad_maximum_fusion, f32[]{:T(128)} %constant.89.clone.1), padding=0_0_0x0_1_1x0_0_0 | pad | bytes 1572868 | tf_op jit(solution)/shard_map/pad | solution.py:64
  119.5 2.0 %pad.131 = f32[2,512,256]{2,1,0:T(8,128)} pad(f32[2,256,256]{2,1,0:T(8,128)S(1)} %add.584, f32[]{:T(128)} %constant.89.clone.1), padding=0_0_0x1_0_1x0_0_0 | pad | bytes 1572868 | tf_op jit(solution)/shard_map/pad | solution.py:64
  121.5 0.7 slice.917
  122.2 0.8 slice.918
  123.0 0.7 slice.854
  123.7 0.7 slice.852
  124.4 2.6 %slice.853 = f32[2,256,256]{2,1,0:T(8,128)} reverse(f32[2,256,256]{2,1,0:T(8,128)S(1)} %slice.852), dimensions={1} | reverse | bytes 1048576 | tf_op jit(solution)/shard_map/slice | solution.py:73
  127.0 2.6 %slice.855 = f32[2,256,256]{2,1,0:T(8,128)} reverse(f32[2,256,256]{2,1,0:T(8,128)S(1)} %slice.854), dimensions={1} | reverse | bytes 1048576 | tf_op jit(solution)/shard_map/slice | solution.py:73
  129.6 1.3 fusion.60
  131.0 0.1 slice.863
  131.1 0.1 slice.859
  131.3 0.2 slice.858
  131.5 0.2 slice.915
  131.7 0.1 slice.861
  131.9 0.1 slice.860
  132.0 0.1 fusion.62
  134.3 0.1 pad.146
  134.4 0.1 pad.147
  134.5 0.9 copy-done.3
  135.4 0.1 fusion.7
  135.6 0.1 add.634
  135.7 0.2 pad.148
  135.9 0.2 pad.149
  136.1 0.1 add.636
  136.3 5.2 %rev.2 = f32[2,512,256]{2,1,0:T(8,128)} reverse(f32[2,512,256]{2,1,0:T(8,128)S(1)} %add.636), dimensions={1} | reverse | bytes 2097152 | tf_op jit(solution)/shard_map/rev | solution.py:73
  141.5 2.5 %fusion.6 = bf16[2,512,256]{2,1,0:T(8,128)(2,1)} fusion(bf16[2,512,256]{2,1,0:T(8,128)(2,1)} %param.9, f32[2,512,256]{2,1,0:T(8,128)} %rev.2, f32[2,512,256]{2,1,0:T(8,128)S(1)} %copy-done.1, f32[2,512,256]{2,1,0:T(8,128)S(1)} %copy-done.2), kind=kLoop, calls=%fused_computation.12 | loop fusion | flops 2359296 | bytes 4194304 | tf_op jit(solution)/shard_map/convert_element_type | solution.py:76
  (200 shorter events, 4.0 us)
Async XLA Ops:
  2.6 13.6 %copy-start = (f32[2,256,4,128]{1,3,2,0:T(8,128)}, f32[2,256,4,128]{1,3,2,0:T(8,128)S(1)}, u32[]{:S(2)}) copy-start(f32[2,256,4,128]{1,3,2,0:T(8,128)S(1)} %copy.53) | copy-start | bytes 3145732
  116.0 1.0 copy-start.5
  116.1 1.1 copy-start.4
  127.0 2.6 %copy-start.6 = (f32[2,256,256]{2,1,0:T(8,128)S(1)}, f32[2,256,256]{2,1,0:T(8,128)}, u32[]{:S(2)}) copy-start(f32[2,256,256]{2,1,0:T(8,128)} %slice.857) | copy-start | bytes 1572868
  127.0 2.6 %copy-start.7 = (f32[2,256,256]{2,1,0:T(8,128)S(1)}, f32[2,256,256]{2,1,0:T(8,128)}, u32[]{:S(2)}) copy-start(f32[2,256,256]{2,1,0:T(8,128)} %slice.851) | copy-start | bytes 1572868
  134.4 1.0 copy-start.3
  136.3 5.2 %copy-start.1 = (f32[2,512,256]{2,1,0:T(8,128)S(1)}, f32[2,512,256]{2,1,0:T(8,128)}, u32[]{:S(2)}) copy-start(f32[2,512,256]{2,1,0:T(8,128)} %pad.130) | copy-start | bytes 3145732
  136.3 5.2 %copy-start.2 = (f32[2,512,256]{2,1,0:T(8,128)S(1)}, f32[2,512,256]{2,1,0:T(8,128)}, u32[]{:S(2)}) copy-start(f32[2,512,256]{2,1,0:T(8,128)} %pad.131) | copy-start | bytes 3145732
where the time goes:
time: 145 us; the launch traced here: 144 us
  blocking collectives  83.7 us (58%)
  local copies, waits for them, and re-layouts  47.4 us (33%)
  other arithmetic  11.6 us (8%)
    all_gather x6, blocking collectives, collected_together(): both, at, found = (lax.all_gather(jnp.concatenate(lines), axis), 0, {})  83.7 us
    slice x56, local copies, waits for them, and re-layouts, local(): lax.associative_scan(join_pair, (keep, started), axis=1, reverse=True)[1]  22.2 us
    slice x52, local copies, waits for them, and re-layouts, local(): forward = lax.associative_scan(join_pair, (keep, started), axis=1)[1]  12 us
    rev x1, local copies, waits for them, and re-layouts, local(): lax.associative_scan(join_pair, (keep, started), axis=1, reverse=True)[1]  5.17 us
    pad x16, local copies, waits for them, and re-layouts, local(): forward = lax.associative_scan(join_pair, (keep, started), axis=1)[1]  4.7 us
    mul x19, other arithmetic, join_pair(): return (earlier[0] * later[0], later[0] * earlier[1] + later[1])  3.05 us

commit v1 on v0

v1 whole, which is shorter than its diff:
```python
import functools

import jax
import jax.numpy as jnp
from jax import lax
from jax.experimental import pallas as pl
from jax.experimental.pallas import tpu as pltpu
from jax.sharding import PartitionSpec as P

MESH = pl.DeviceIdType.MESH
INNER = 8
LANES = 128


def triangle(rows, upper):
    r = lax.broadcasted_iota(jnp.int32, (rows, rows), 0)
    c = lax.broadcasted_iota(jnp.int32, (rows, rows), 1)
    inside = c >= r if upper else c <= r
    return jnp.where(inside, 1.0, 0.0).astype(jnp.bfloat16)


def running(mask, value):
    high = value.astype(jnp.bfloat16)
    low = (value - high.astype(jnp.float32)).astype(jnp.bfloat16)
    dot = functools.partial(jnp.dot, preferred_element_type=jnp.float32)
    return dot(mask, high) + dot(mask, low)


def kernel(
    outer, total_length, rows,
    fade_h, upd_h, gate_h, out_ref,
    fade_v, upd_v, gate_v, lower, upper, logs, base, qv, rv,
    row_out, row_in, far_out, far_in,
    load_sem, row_send, row_recv, far_send, far_recv,
):
    batch, length, width = fade_v.shape
    parts = length // rows
    tiles = width // LANES
    quantity = batch * tiles
    seq = lax.axis_index("seq")
    z, r = seq // INNER, seq % INNER

    def row_peer(d):
        return (r + d) % INNER

    def far_peer(d):
        return (z + d) % outer

    def order(count):
        return sorted(range(1, count), key=lambda d: -min(d, count - d))

    barrier = pltpu.get_barrier_semaphore()
    for d in order(outer):
        pl.semaphore_signal(
            barrier, inc=1, device_id={"seq": far_peer(d) * INNER + r}, device_id_type=MESH
        )
    for d in order(INNER):
        pl.semaphore_signal(
            barrier, inc=1, device_id={"seq": z * INNER + row_peer(d)}, device_id_type=MESH
        )

    loads = {}
    for k, (src, dst) in enumerate(((fade_h, fade_v), (upd_h, upd_v), (gate_h, gate_v))):
        for b in range(batch):
            for p in range(parts):
                at = (b, pl.ds(p * rows, rows))
                loads[k, b, p] = pltpu.make_async_copy(
                    src.at[at], dst.at[at], load_sem.at[k, b, p]
                )
    for k in range(3):
        for b in range(batch):
            for p in range(parts):
                loads[k, b, p].start()

    lower[...] = triangle(rows, False)
    upper[...] = triangle(rows, True)
    scale = 1.0 / total_length

    for b in range(batch):
        passed = jnp.zeros((1, width), jnp.float32)
        sums = jnp.zeros((1, width), jnp.float32)
        back = jnp.zeros((1, width), jnp.float32)
        for p in range(parts):
            at = (b, slice(p * rows, (p + 1) * rows))
            loads[0, b, p].wait()
            fade = fade_v[at]
            log = running(lower[...], fade) + passed
            logs[at] = log
            loads[1, b, p].wait()
            push = upd_v[at].astype(jnp.float32)
            sums = sums + jnp.sum(jnp.exp(log * scale) * push, axis=0, keepdims=True)
            back = back + jnp.sum(jnp.exp((fade - log) * scale) * push, axis=0, keepdims=True)
            passed = log[rows - 1 :, :]
        keep = jnp.exp(-passed * scale)
        for t in range(tiles):
            i, cut = b * tiles + t, slice(t * LANES, (t + 1) * LANES)
            row_out[i : i + 1, :] = keep[:, cut]
            row_out[quantity + i : quantity + i + 1, :] = (keep * sums)[:, cut]
            row_out[2 * quantity + i : 2 * quantity + i + 1, :] = back[:, cut]

    pl.semaphore_wait(barrier, outer - 1 + INNER - 1)
    row_copies = []
    for d in order(INNER):
        row_copies.append(
            pltpu.make_async_remote_copy(
                src_ref=row_out,
                dst_ref=row_in.at[r],
                send_sem=row_send.at[d],
                recv_sem=row_recv.at[r],
                device_id={"seq": z * INNER + row_peer(d)},
                device_id_type=MESH,
            )
        )
        row_copies[-1].start()

    for b in range(batch):
        passed = jnp.zeros((1, width), jnp.float32)
        for p in range(parts):
            at = (b, slice(p * rows, (p + 1) * rows))
            log = logs[at]
            push = upd_v[at].astype(jnp.float32)
            run = running(lower[...], jnp.exp(log * scale) * push) + passed
            passed = run[rows - 1 :, :]
            base[at] = run * jnp.exp(-log * scale)

    own = row_out[...]
    row_in[pl.ds(r, 1)] = own[None]
    for d in range(1, INNER):
        slot = row_peer(d)
        pltpu.make_async_remote_copy(
            src_ref=row_out,
            dst_ref=row_in.at[slot],
            send_sem=row_send.at[d],
            recv_sem=row_recv.at[slot],
            device_id={"seq": z * INNER + slot},
            device_id_type=MESH,
        ).wait_recv()

    def parts_of(share):
        return share[:quantity], share[quantity : 2 * quantity], share[2 * quantity :]

    shares = [parts_of(row_in[k]) for k in range(INNER)]
    zero, one = jnp.zeros((quantity, LANES), jnp.float32), jnp.ones((quantity, LANES), jnp.float32)
    keep_row, forward_row, backward_row = one, zero, zero
    keep_before, forward_before = one, zero
    for k in range(INNER):
        keep, forward, _ = shares[k]
        forward_row = keep * forward_row + forward
        keep_row = keep * keep_row
        keep_before = jnp.where(k < r, keep_row, keep_before)
        forward_before = jnp.where(k < r, forward_row, forward_before)
    keep_part, keep_after, backward_after = one, one, zero
    for k in reversed(range(INNER)):
        keep, _, backward = shares[k]
        backward_row = keep * backward_row + backward
        keep_part = keep * keep_part
        keep_after = jnp.where(k > r, keep_part, keep_after)
        backward_after = jnp.where(k > r, backward_row, backward_after)
    for k, last in enumerate((forward_row, backward_row)):
        far_out[k, :quantity] = keep_row
        far_out[k, quantity:] = last

    far_copies = []
    for d in order(outer):
        way = jnp.where(far_peer(d) > z, 0, 1)
        far_copies.append(
            pltpu.make_async_remote_copy(
                src_ref=far_out.at[way],
                dst_ref=far_in.at[z],
                send_sem=far_send.at[d],
                recv_sem=far_recv.at[z],
                device_id={"seq": far_peer(d) * INNER + r},
                device_id_type=MESH,
            )
        )
        far_copies[-1].start()

    own_keep = own[:quantity]
    for b in range(batch):
        passed = jnp.zeros((1, width), jnp.float32)
        for p in reversed(range(parts)):
            at = (b, slice(p * rows, (p + 1) * rows))
            log = logs[at]
            before = log - fade_v[at]
            push = upd_v[at].astype(jnp.float32)
            run = running(upper[...], jnp.exp(-before * scale) * push) + passed
            passed = run[:1, :]
            loads[2, b, p].wait()
            gate = gate_v[at].astype(jnp.float32)
            gate = gate * (total_length**-0.5) / (1.0 + jnp.exp(-gate))
            raised = jnp.exp(before * scale) * gate
            base[at] = base[at] * gate + run * raised
            qv[at] = jnp.exp(-log * scale) * gate
            rv[at] = raised

    far_in[pl.ds(z, 1)] = far_out[0:1]
    for d in range(1, outer):
        slot = far_peer(d)
        pltpu.make_async_remote_copy(
            src_ref=far_out.at[0],
            dst_ref=far_in.at[slot],
            send_sem=far_send.at[d],
            recv_sem=far_recv.at[slot],
            device_id={"seq": slot * INNER + r},
            device_id_type=MESH,
        ).wait_recv()
    enter_forward, enter_backward = zero, zero
    for k in range(outer):
        share = far_in[k]
        new = share[:quantity] * enter_forward + share[quantity:]
        enter_forward = jnp.where(k < z, new, enter_forward)
    for k in reversed(range(outer)):
        share = far_in[k]
        new = share[:quantity] * enter_backward + share[quantity:]
        enter_backward = jnp.where(k > z, new, enter_backward)
    enter_forward = keep_before * enter_forward + forward_before
    enter_backward = own_keep * (keep_after * enter_backward + backward_after)

    for b in range(batch):
        for t in range(tiles):
            i, cut = b * tiles + t, slice(t * LANES, (t + 1) * LANES)
            ahead, behind = enter_forward[i : i + 1], enter_backward[i : i + 1]
            out_ref[b, :, cut] = (
                base[b, :, cut] + qv[b, :, cut] * ahead + rv[b, :, cut] * behind
            ).astype(out_ref.dtype)

    for copy in row_copies + far_copies:
        copy.wait_send()


def local(outer, total_length, fade_rate, update_in, gate_in):
    batch, length, width = fade_rate.shape
    rows = min(256, length)
    parts = length // rows
    quantity = batch * width // LANES
    full, f32 = (batch, length, width), jnp.float32
    return pl.pallas_call(
        functools.partial(kernel, outer, total_length, rows),
        out_shape=jax.ShapeDtypeStruct(full, update_in.dtype),
        in_specs=[pl.BlockSpec(memory_space=pltpu.HBM)] * 3,
        out_specs=pl.BlockSpec(memory_space=pltpu.VMEM),
        scratch_shapes=[
            pltpu.VMEM(full, f32),
            pltpu.VMEM(full, update_in.dtype),
            pltpu.VMEM(full, gate_in.dtype),
            pltpu.VMEM((rows, rows), jnp.bfloat16),
            pltpu.VMEM((rows, rows), jnp.bfloat16),
            pltpu.VMEM(full, f32),
            pltpu.VMEM(full, f32),
            pltpu.VMEM(full, f32),
            pltpu.VMEM(full, f32),
            pltpu.VMEM((3 * quantity, LANES), f32),
            pltpu.VMEM((INNER, 3 * quantity, LANES), f32),
            pltpu.VMEM((2, 2 * quantity, LANES), f32),
            pltpu.VMEM((outer, 2 * quantity, LANES), f32),
            pltpu.SemaphoreType.DMA((3, batch, parts)),
            pltpu.SemaphoreType.DMA((INNER,)),
            pltpu.SemaphoreType.DMA((INNER,)),
            pltpu.SemaphoreType.DMA((outer,)),
            pltpu.SemaphoreType.DMA((outer,)),
        ],
        compiler_params=pltpu.CompilerParams(
            collective_id=0, has_side_effects=True, vmem_limit_bytes=32 * 2**20
        ),
    )(*(pltpu.with_memory_space_constraint(a, pltpu.HBM) for a in (fade_rate, update_in, gate_in)))


def solution(mesh):
    spec = P(None, "seq", "width")
    devices = mesh.shape["seq"]

    def step(fade_rate, update_in, gate_in):
        body = functools.partial(local, devices // INNER, fade_rate.shape[1])
        return jax.shard_map(
            body, mesh=mesh, in_specs=(spec, spec, spec), out_specs=spec, check_vma=False
        )(fade_rate, update_in, gate_in)

    return step
```

time: 145 us -> 21.4 us (0.15)
  the two profiles are of different devices: /device:TPU:8 before, /device:TPU:1 now
where the time goes in v1:
time: 21.4 us; the launch traced here: 21.3 us
  Pallas kernels  20.5 us (96%)
  local copies, waits for them, and re-layouts  0.8 us (4%)
    pallas_call x1, Pallas kernels, local(): pl.pallas_call(functools.partial(kernel, outer, total_length, rows), out_...  20.5 us
    unnamed x1, local copies, waits for them, and re-layouts  0.8 us

profile of v1, /device:TPU:1, one launch (start us, length us, event | category | flops | bytes accessed | tf_op | source)
XLA Modules:
  0.0 21.3 jit_solution(16829662684047615930)
XLA Ops:
  0.0 20.5 %shard_map.37 = bf16[2,512,256]{2,1,0:T(8,128)(2,1)S(1)} custom-call(f32[2,512,256]{2,1,0:T(8,128)} %fade_h.1, bf16[2,512,256]{2,1,0:T(8,128)(2,1)} %upd_h.1, bf16[2,512,256]{2,1,0:T(8,128)(2,1)} %gate_h.1), custom_call_target="tpu_custom_call" | custom-call | tf_op jit(solution)/shard_map/pallas_call | solution.py:237
  20.5 0.8 %copy.5 = bf16[2,512,256]{2,1,0:T(8,128)(2,1)} copy(bf16[2,512,256]{2,1,0:T(8,128)(2,1)S(1)} %shard_map.37) | data formatting | bytes 1048576

commit v2 on v1

v2 whole, which is shorter than its diff:
```python
import functools
import math

import jax
import jax.numpy as jnp
from jax import lax
from jax.experimental import pallas as pl
from jax.experimental.pallas import tpu as pltpu
from jax.sharding import PartitionSpec as P

MESH = pl.DeviceIdType.MESH
INNER = 8
LANES = 128
ROWS = 128
SUB = 8


def triangle(rows, upper):
    r = lax.broadcasted_iota(jnp.int32, (rows, rows), 0)
    c = lax.broadcasted_iota(jnp.int32, (rows, rows), 1)
    inside = c >= r if upper else c <= r
    return jnp.where(inside, 1.0, 0.0).astype(jnp.bfloat16)


dot = functools.partial(jnp.dot, preferred_element_type=jnp.float32)


def running(mask, value):
    high = value.astype(jnp.bfloat16)
    low = (value - high.astype(jnp.float32)).astype(jnp.bfloat16)
    return dot(mask, high) + dot(mask, low)


def folded(value):
    return jnp.sum(value.reshape(value.shape[0] // SUB, SUB, value.shape[1]), axis=0)


def kernel(
    outer, total_length,
    fade_h, upd_h, gate_h, out_ref,
    fade_v, upd_v, gate_v, lower, upper, logs, base, qv, rv, into,
    row_out, row_in, far_out, far_in,
    load_sem, row_send, row_recv, far_send, far_recv, near_sem, next_sem,
):
    batch, length, width = fade_v.shape
    parts = length // ROWS
    tiles = width // LANES
    quantity = batch * tiles
    seq = lax.axis_index("seq")
    z, r = seq // INNER, seq % INNER

    def row_peer(d):
        return {"seq": z * INNER + (r + d) % INNER}

    def far_peer(d):
        return {"seq": ((z + d) % outer) * INNER + r}

    def order(count):
        return sorted(range(1, count), key=lambda d: -min(d, count - d))

    def signal(sem, peer):
        pl.semaphore_signal(sem, inc=1, device_id=peer, device_id_type=MESH)

    half = length // 2
    arrays = ((fade_h, fade_v), (upd_h, upd_v), (gate_h, gate_v))
    for b in range(batch):
        for k in range(2):
            for h in range(2):
                at = (b, pl.ds(h * half, half))
                src, dst = arrays[k]
                pltpu.make_async_copy(src.at[at], dst.at[at], load_sem.at[k, b]).start()

    def loaded(k, b):
        src, dst = arrays[k]
        pltpu.make_async_copy(src.at[b], dst.at[b], load_sem.at[k, b]).wait()

    barrier = pltpu.get_barrier_semaphore()
    for d in order(INNER):
        signal(barrier, row_peer(d))
    for d in (1, outer - 1):
        signal(barrier, far_peer(d))
    for b in range(batch):
        src, dst = arrays[2]
        pltpu.make_async_copy(src.at[b], dst.at[b], load_sem.at[2, b]).start()

    lower[...] = triangle(ROWS, False)
    scale = math.log2(math.e) / total_length

    totals = {}
    for b in range(batch):
        loaded(0, b)
        loaded(1, b)
        ups, downs = [], []
        for p in range(parts):
            at = (b, slice(p * ROWS, (p + 1) * ROWS))
            fade = fade_v[at]
            log = dot(lower[...], fade.astype(jnp.bfloat16))
            logs[at] = log
            push = upd_v[at].astype(jnp.float32)
            ups.append(folded(jnp.exp2(log * scale) * push))
            downs.append(folded(jnp.exp2((fade - log) * scale) * push))
            total = jnp.sum(folded(fade), axis=0, keepdims=True)
            totals[b, p] = total
        keeps = [jnp.exp2(totals[b, p] * -scale) for p in range(parts)]
        state = jnp.zeros((SUB, width), jnp.float32)
        for p in range(parts):
            into[0, b, p] = state
            state = keeps[p] * (state + ups[p])
        forward = jnp.sum(state, axis=0, keepdims=True)
        state = jnp.zeros((SUB, width), jnp.float32)
        for p in reversed(range(parts)):
            into[1, b, p] = keeps[p] * state
            state = downs[p] + keeps[p] * state
        backward = jnp.sum(state, axis=0, keepdims=True)
        keep = jnp.exp2(sum(totals[b, p] for p in range(parts)) * -scale)
        for t in range(tiles):
            i, cut = b * tiles + t, slice(t * LANES, (t + 1) * LANES)
            row_out[i : i + 1, :] = keep[:, cut]
            row_out[quantity + i : quantity + i + 1, :] = forward[:, cut]
            row_out[2 * quantity + i : 2 * quantity + i + 1, :] = backward[:, cut]

    pl.semaphore_wait(barrier, INNER - 1 + 2)
    for d in order(INNER):
        pltpu.make_async_remote_copy(
            src_ref=row_out, dst_ref=row_in.at[r], send_sem=row_send, recv_sem=row_recv,
            device_id=row_peer(d), device_id_type=MESH,
        ).start()
    for d in (1, outer - 1):
        signal(near_sem, far_peer(d))

    upper[...] = triangle(ROWS, True)

    def forward_part(b):
        for p in range(parts):
            at = (b, slice(p * ROWS, (p + 1) * ROWS))
            log = logs[at] * scale
            push = upd_v[at].astype(jnp.float32)
            enter = jnp.sum(into[0, b, p], axis=0, keepdims=True)
            run = running(lower[...], jnp.exp2(log) * push) + enter
            base[at] = run * jnp.exp2(-log)

    forward_part(0)
    pl.semaphore_wait(near_sem, 2)
    for d in (2, outer - 2):
        signal(next_sem, far_peer(d))
    for b in range(1, batch):
        forward_part(b)

    own = row_out[...]
    row_in[pl.ds(r, 1)] = own[None]
    others = row_in.at[pl.ds(0, INNER - 1)]
    pltpu.make_async_copy(others, others, row_recv).wait()

    def parts_of(share):
        return share[:quantity], share[quantity : 2 * quantity], share[2 * quantity :]

    shares = [parts_of(row_in[k]) for k in range(INNER)]
    zero, one = jnp.zeros((quantity, LANES), jnp.float32), jnp.ones((quantity, LANES), jnp.float32)
    keep_row, forward_row, backward_row = one, zero, zero
    keep_before, forward_before = one, zero
    for k in range(INNER):
        keep, forward, _ = shares[k]
        forward_row = keep * forward_row + forward
        keep_row = keep * keep_row
        keep_before = jnp.where(k < r, keep_row, keep_before)
        forward_before = jnp.where(k < r, forward_row, forward_before)
    keep_part, keep_after, backward_after = one, one, zero
    for k in reversed(range(INNER)):
        keep, _, backward = shares[k]
        backward_row = keep * backward_row + backward
        keep_part = keep * keep_part
        keep_after = jnp.where(k > r, keep_part, keep_after)
        backward_after = jnp.where(k > r, backward_row, backward_after)
    for k, last in enumerate((forward_row, backward_row)):
        far_out[k, :quantity] = keep_row
        far_out[k, quantity:] = last

    pl.semaphore_wait(next_sem, 2)
    for d in order(outer):
        way = jnp.where((z + d) % outer > z, 0, 1)
        pltpu.make_async_remote_copy(
            src_ref=far_out.at[way], dst_ref=far_in.at[z], send_sem=far_send, recv_sem=far_recv,
            device_id=far_peer(d), device_id_type=MESH,
        ).start()

    for b in range(batch):
        loaded(2, b)
        before = jnp.zeros((1, width), jnp.float32)
        for p in range(parts):
            at = (b, slice(p * ROWS, (p + 1) * ROWS))
            log = logs[at] * scale
            short = log - fade_v[at] * scale
            push = upd_v[at].astype(jnp.float32)
            enter = jnp.sum(into[1, b, p], axis=0, keepdims=True)
            run = running(upper[...], jnp.exp2(-short) * push) + enter
            gate = gate_v[at].astype(jnp.float32)
            gate = gate * (total_length**-0.5) / (1.0 + jnp.exp(-gate))
            raised = jnp.exp2(short) * gate
            base[at] = base[at] * gate + run * raised
            after = sum(totals[b, q] for q in range(p, parts))
            qv[at] = jnp.exp2(-log) * gate * jnp.exp2(before * -scale)
            rv[at] = raised * jnp.exp2(after * -scale)
            before = before + totals[b, p]

    far_in[pl.ds(z, 1)] = far_out[0:1]
    others = far_in.at[pl.ds(0, outer - 1)]
    pltpu.make_async_copy(others, others, far_recv).wait()
    enter_forward, enter_backward = zero, zero
    for k in range(outer):
        share = far_in[k]
        new = share[:quantity] * enter_forward + share[quantity:]
        enter_forward = jnp.where(k < z, new, enter_forward)
    for k in reversed(range(outer)):
        share = far_in[k]
        new = share[:quantity] * enter_backward + share[quantity:]
        enter_backward = jnp.where(k > z, new, enter_backward)
    enter_forward = keep_before * enter_forward + forward_before
    enter_backward = keep_after * enter_backward + backward_after

    for b in range(batch):
        for t in range(tiles):
            i, cut = b * tiles + t, slice(t * LANES, (t + 1) * LANES)
            ahead, behind = enter_forward[i : i + 1], enter_backward[i : i + 1]
            out_ref[b, :, cut] = (
                base[b, :, cut] + qv[b, :, cut] * ahead + rv[b, :, cut] * behind
            ).astype(out_ref.dtype)

    for refs, count, sem in ((row_in, INNER, row_send), (far_in, outer, far_send)):
        sent = refs.at[pl.ds(0, count - 1)]
        pltpu.make_async_copy(sent, sent, sem).wait()


def local(outer, total_length, fade_rate, update_in, gate_in):
    batch, length, width = fade_rate.shape
    quantity = batch * width // LANES
    full, f32 = (batch, length, width), jnp.float32
    arguments = (fade_rate, update_in, gate_in)
    return pl.pallas_call(
        functools.partial(kernel, outer, total_length),
        out_shape=jax.ShapeDtypeStruct(full, update_in.dtype),
        in_specs=[pl.BlockSpec(memory_space=pltpu.HBM)] * 3,
        out_specs=pl.BlockSpec(memory_space=pltpu.VMEM),
        scratch_shapes=[
            pltpu.VMEM(full, f32),
            pltpu.VMEM(full, update_in.dtype),
            pltpu.VMEM(full, gate_in.dtype),
            pltpu.VMEM((ROWS, ROWS), jnp.bfloat16),
            pltpu.VMEM((ROWS, ROWS), jnp.bfloat16),
            pltpu.VMEM(full, f32),
            pltpu.VMEM(full, f32),
            pltpu.VMEM(full, f32),
            pltpu.VMEM(full, f32),
            pltpu.VMEM((2, batch, length // ROWS, SUB, width), f32),
            pltpu.VMEM((3 * quantity, LANES), f32),
            pltpu.VMEM((INNER, 3 * quantity, LANES), f32),
            pltpu.VMEM((2, 2 * quantity, LANES), f32),
            pltpu.VMEM((outer, 2 * quantity, LANES), f32),
            pltpu.SemaphoreType.DMA((3, batch)),
            pltpu.SemaphoreType.DMA,
            pltpu.SemaphoreType.DMA,
            pltpu.SemaphoreType.DMA,
            pltpu.SemaphoreType.DMA,
            pltpu.SemaphoreType.REGULAR,
            pltpu.SemaphoreType.REGULAR,
        ],
        compiler_params=pltpu.CompilerParams(
            collective_id=0, has_side_effects=True, vmem_limit_bytes=32 * 2**20
        ),
    )(*(pltpu.with_memory_space_constraint(a, pltpu.HBM) for a in arguments))


def solution(mesh):
    spec = P(None, "seq", "width")
    devices = mesh.shape["seq"]

    def step(fade_rate, update_in, gate_in):
        body = functools.partial(local, devices // INNER, fade_rate.shape[1])
        return jax.shard_map(
            body, mesh=mesh, in_specs=(spec, spec, spec), out_specs=spec, check_vma=False
        )(fade_rate, update_in, gate_in)

    return step
```

time: 21.4 us -> 19.8 us (0.925)
  Pallas kernels: 20.5 us -> 18.9 us
    pallas_call x1, Pallas kernels: 20.5 us -> 18.9 us  [local(): pl.pallas_call(functools.partial(kernel, outer, total_length), out_shape=...]
where the time goes in v2:
time: 19.8 us; the launch traced here: 19.7 us
  Pallas kernels  18.9 us (95%)
  local copies, waits for them, and re-layouts  0.8 us (4%)
    pallas_call x1, Pallas kernels, local(): pl.pallas_call(functools.partial(kernel, outer, total_length), out_shape=...  18.9 us
    unnamed x1, local copies, waits for them, and re-layouts  0.8 us

profile of v2, /device:TPU:1, one launch (start us, length us, event | category | flops | bytes accessed | tf_op | source)
XLA Modules:
  0.0 19.7 jit_solution(10967018547207621740)
XLA Ops:
  0.0 18.9 %shard_map.37 = bf16[2,512,256]{2,1,0:T(8,128)(2,1)S(1)} custom-call(f32[2,512,256]{2,1,0:T(8,128)} %fade_h.1, bf16[2,512,256]{2,1,0:T(8,128)(2,1)} %upd_h.1, bf16[2,512,256]{2,1,0:T(8,128)(2,1)} %gate_h.1), custom_call_target="tpu_custom_call" | custom-call | tf_op jit(solution)/shard_map/pallas_call | solution.py:238
  18.9 0.8 %copy.5 = bf16[2,512,256]{2,1,0:T(8,128)(2,1)} copy(bf16[2,512,256]{2,1,0:T(8,128)(2,1)S(1)} %shard_map.37) | data formatting | bytes 1048576

commit v3 on v2

v3 whole, which is shorter than its diff:
```python
import functools
import math

import jax
import jax.numpy as jnp
from jax import lax
from jax.experimental import pallas as pl
from jax.experimental.pallas import tpu as pltpu
from jax.sharding import PartitionSpec as P

MESH = pl.DeviceIdType.MESH
INNER = 8
CORES = 2
CHIPS = INNER // CORES
LANES = 128
ROWS = 128
SUB = 8


def triangle(rows, upper):
    r = lax.broadcasted_iota(jnp.int32, (rows, rows), 0)
    c = lax.broadcasted_iota(jnp.int32, (rows, rows), 1)
    inside = c >= r if upper else c <= r
    return jnp.where(inside, 1.0, 0.0).astype(jnp.bfloat16)


dot = functools.partial(jnp.dot, preferred_element_type=jnp.float32)


def running(mask, value):
    high = value.astype(jnp.bfloat16)
    low = (value - high.astype(jnp.float32)).astype(jnp.bfloat16)
    return dot(mask, high) + dot(mask, low)


def folded(value):
    return jnp.sum(value.reshape(value.shape[0] // SUB, SUB, value.shape[1]), axis=0)


def kernel(
    outer, total_length,
    fade_h, upd_h, gate_h, out_ref,
    fade_v, upd_v, gate_v, lower, upper, logs, base, qv, rv, into,
    row_out, row_in, far_out, far_in,
    load_sem, gate_sem, row_send, row_recv, far_send, far_recv, told,
):
    batch, length, width = upd_v.shape
    parts = length // ROWS
    tiles = width // LANES
    seq = lax.axis_index("seq")
    z, r = seq // INNER, seq % INNER
    x, core = r // CORES, r % CORES

    def at(row, place):
        return {"seq": row * INNER + place}

    def others(own, count):
        return [k + jnp.where(k >= own, 1, 0) for k in range(count - 1)]

    def signal(sem, peer):
        pl.semaphore_signal(sem, inc=1, device_id=peer, device_id_type=MESH)

    def send(src, dst, out_sem, in_sem, peer):
        pltpu.make_async_remote_copy(
            src_ref=src, dst_ref=dst, send_sem=out_sem, recv_sem=in_sem,
            device_id=peer, device_id_type=MESH,
        ).start()

    def wait(ref, sem):
        pltpu.make_async_copy(ref, ref, sem).wait()

    def load(b):
        half = length // 2
        for h in range(2):
            part = pl.ds(h * half, half)
            to = fade_v.at[pl.ds(b * length + h * half, half)]
            pltpu.make_async_copy(fade_h.at[b, part], to, load_sem.at[b]).start()
            to = upd_v.at[b, part]
            pltpu.make_async_copy(upd_h.at[b, part], to, load_sem.at[b]).start()

    def loaded(b):
        wait(fade_v.at[pl.ds(0, length + length // 2)], load_sem.at[b])

    load(0)
    barrier = pltpu.get_barrier_semaphore()
    for d in range(1, CHIPS):
        signal(barrier, at(z, (x + d) % CHIPS * CORES + 1))

    @pl.when(core == 0)
    def _():
        signal(barrier, at(z, r + 1))

    load(1)
    for row in others(z, outer):
        signal(barrier, at(row, x * CORES))
    lower[...] = triangle(ROWS, False)
    scale = math.log2(math.e) / total_length
    partner = at(z, r + 1 - 2 * core)

    totals = {}

    def summary(b):
        ups, downs = [], []
        for p in range(parts):
            cut = (b, slice(p * ROWS, (p + 1) * ROWS))
            fade = fade_v[b * length + p * ROWS : b * length + (p + 1) * ROWS] * scale
            log = dot(lower[...], fade.astype(jnp.bfloat16))
            logs[cut] = log
            push = upd_v[cut].astype(jnp.float32)
            ups.append(folded(jnp.exp2(log) * push))
            downs.append(folded(jnp.exp2(fade - log) * push))
            totals[b, p] = jnp.sum(folded(fade), axis=0, keepdims=True)
        keeps = [jnp.exp2(-totals[b, p]) for p in range(parts)]
        state = jnp.zeros((SUB, width), jnp.float32)
        for p in range(parts):
            into[0, b, p] = state
            state = keeps[p] * (state + ups[p])
        forward = jnp.sum(state, axis=0, keepdims=True)
        state = jnp.zeros((SUB, width), jnp.float32)
        for p in reversed(range(parts)):
            into[1, b, p] = keeps[p] * state
            state = downs[p] + keeps[p] * state
        backward = jnp.sum(state, axis=0, keepdims=True)
        keep = jnp.exp2(-sum(totals[b, p] for p in range(parts)))
        for k, value in enumerate((keep, forward, backward)):
            for t in range(tiles):
                i = k * tiles + t
                row_out[b, i : i + 1, :] = value[:, t * LANES : (t + 1) * LANES]

    def send_row(b):
        own = (1 - core) * CHIPS + x
        for k in others(own, INNER):
            place = k % CHIPS * CORES + 1 - k // CHIPS
            send(row_out.at[b], row_in.at[b, r], row_send.at[b], row_recv.at[b], at(z, place))

    loaded(0)
    summary(0)

    @pl.when(core == 1)
    def _():
        pl.semaphore_wait(barrier, INNER - 1)
        signal(told, partner)

    @pl.when(core == 0)
    def _():
        pl.semaphore_wait(told, 1)

    send_row(0)
    for b in range(1, batch):
        loaded(b)
        if b == batch - 1:
            pltpu.make_async_copy(gate_h, gate_v, gate_sem).start()
        summary(b)
        send_row(b)

    upper[...] = triangle(ROWS, True)

    for b in range(batch):
        for p in range(parts):
            cut = (b, slice(p * ROWS, (p + 1) * ROWS))
            log = logs[cut]
            push = upd_v[cut].astype(jnp.float32)
            enter = jnp.sum(into[0, b, p], axis=0, keepdims=True)
            run = running(lower[...], jnp.exp2(log) * push) + enter
            base[cut] = run * jnp.exp2(-log)

    @pl.when(core == 0)
    def _():
        pl.semaphore_wait(barrier, CORES * (outer - 1))
        signal(told, partner)

    @pl.when(core == 1)
    def _():
        pl.semaphore_wait(told, 1)

    zero, one = jnp.zeros((tiles, LANES), jnp.float32), jnp.ones((tiles, LANES), jnp.float32)

    def combine_row(b):
        row_in[b, pl.ds(r, 1)] = row_out[b][None]
        wait(row_in.at[b, pl.ds(0, INNER - 1)], row_recv.at[b])
        shares = [row_in[b, k] for k in range(INNER)]
        shares = [(s[:tiles], s[tiles : 2 * tiles], s[2 * tiles :]) for s in shares]
        keep_row, forward_row, backward_row = one, zero, zero
        keep_before, forward_before = one, zero
        for k in range(INNER):
            keep, forward, _ = shares[k]
            forward_row = keep * forward_row + forward
            keep_row = keep * keep_row
            keep_before = jnp.where(k < r, keep_row, keep_before)
            forward_before = jnp.where(k < r, forward_row, forward_before)
        keep_part, keep_after, backward_after = one, one, zero
        for k in reversed(range(INNER)):
            keep, _, backward = shares[k]
            backward_row = keep * backward_row + backward
            keep_part = keep * keep_part
            keep_after = jnp.where(k > r, keep_part, keep_after)
            backward_after = jnp.where(k > r, backward_row, backward_after)
        for k, last in enumerate((forward_row, backward_row)):
            far_out[b, k, :tiles] = keep_row
            far_out[b, k, tiles:] = last

        @pl.when(core == 1)
        def _():
            for row in others(z, outer):
                way = jnp.where(row > z, 0, 1)
                for c in (1, 0):
                    send(
                        far_out.at[b, way], far_in.at[b, z], far_send, far_recv.at[b],
                        at(row, x * CORES + c),
                    )

        return keep_before, forward_before, keep_after, backward_after

    inside = [combine_row(b) for b in range(batch)]

    wait(gate_v, gate_sem)
    for b in range(batch):
        before = jnp.zeros((1, width), jnp.float32)
        for p in range(parts):
            cut = (b, slice(p * ROWS, (p + 1) * ROWS))
            log = logs[cut]
            short = log - fade_v[b * length + p * ROWS : b * length + (p + 1) * ROWS] * scale
            push = upd_v[cut].astype(jnp.float32)
            enter = jnp.sum(into[1, b, p], axis=0, keepdims=True)
            run = running(upper[...], jnp.exp2(-short) * push) + enter
            gate = gate_v[cut].astype(jnp.float32)
            gate = gate * (total_length**-0.5) / (1.0 + jnp.exp(-gate))
            raised = jnp.exp2(short) * gate
            base[cut] = base[cut] * gate + run * raised
            after = sum(totals[b, q] for q in range(p, parts))
            qv[cut] = jnp.exp2(-log) * gate * jnp.exp2(-before)
            rv[cut] = raised * jnp.exp2(-after)
            before = before + totals[b, p]

    for b in range(batch):
        far_in[b, pl.ds(z, 1)] = far_out[b, 0:1]
        wait(far_in.at[b, pl.ds(0, outer - 1)], far_recv.at[b])
        keep_before, forward_before, keep_after, backward_after = inside[b]
        shares = [far_in[b, k] for k in range(outer)]
        enter_forward, enter_backward = zero, zero
        for k in range(outer):
            new = shares[k][:tiles] * enter_forward + shares[k][tiles:]
            enter_forward = jnp.where(k < z, new, enter_forward)
        for k in reversed(range(outer)):
            new = shares[k][:tiles] * enter_backward + shares[k][tiles:]
            enter_backward = jnp.where(k > z, new, enter_backward)
        enter_forward = keep_before * enter_forward + forward_before
        enter_backward = keep_after * enter_backward + backward_after
        for t in range(tiles):
            cut = slice(t * LANES, (t + 1) * LANES)
            ahead, behind = enter_forward[t : t + 1], enter_backward[t : t + 1]
            out_ref[b, :, cut] = (
                base[b, :, cut] + qv[b, :, cut] * ahead + rv[b, :, cut] * behind
            ).astype(out_ref.dtype)

    for b in range(batch):
        wait(row_in.at[b, pl.ds(0, INNER - 1)], row_send.at[b])

    @pl.when(core == 1)
    def _():
        sent = batch * CORES * (outer - 1) * 2 * tiles * LANES // width
        wait(fade_v.at[pl.ds(0, sent)], far_send)


def local(outer, total_length, fade_rate, update_in, gate_in):
    batch, length, width = fade_rate.shape
    tiles = width // LANES
    full, f32 = (batch, length, width), jnp.float32
    arguments = (fade_rate, update_in, gate_in)
    return pl.pallas_call(
        functools.partial(kernel, outer, total_length),
        out_shape=jax.ShapeDtypeStruct(full, update_in.dtype),
        in_specs=[pl.BlockSpec(memory_space=pltpu.HBM)] * 3,
        out_specs=pl.BlockSpec(memory_space=pltpu.VMEM),
        scratch_shapes=[
            pltpu.VMEM((batch * length, width), f32),
            pltpu.VMEM(full, update_in.dtype),
            pltpu.VMEM(full, gate_in.dtype),
            pltpu.VMEM((ROWS, ROWS), jnp.bfloat16),
            pltpu.VMEM((ROWS, ROWS), jnp.bfloat16),
            pltpu.VMEM(full, f32),
            pltpu.VMEM(full, f32),
            pltpu.VMEM(full, f32),
            pltpu.VMEM(full, f32),
            pltpu.VMEM((2, batch, length // ROWS, SUB, width), f32),
            pltpu.VMEM((batch, 3 * tiles, LANES), f32),
            pltpu.VMEM((batch, INNER, 3 * tiles, LANES), f32),
            pltpu.VMEM((batch, 2, 2 * tiles, LANES), f32),
            pltpu.VMEM((batch, outer, 2 * tiles, LANES), f32),
            pltpu.SemaphoreType.DMA((batch,)),
            pltpu.SemaphoreType.DMA,
            pltpu.SemaphoreType.DMA((batch,)),
            pltpu.SemaphoreType.DMA((batch,)),
            pltpu.SemaphoreType.DMA,
            pltpu.SemaphoreType.DMA((batch,)),
            pltpu.SemaphoreType.REGULAR,
        ],
        compiler_params=pltpu.CompilerParams(
            collective_id=0, has_side_effects=True, vmem_limit_bytes=32 * 2**20
        ),
    )(*(pltpu.with_memory_space_constraint(a, pltpu.HBM) for a in arguments))


def solution(mesh):
    spec = P(None, "seq", "width")
    devices = mesh.shape["seq"]

    def step(fade_rate, update_in, gate_in):
        body = functools.partial(local, devices // INNER, fade_rate.shape[1])
        return jax.shard_map(
            body, mesh=mesh, in_specs=(spec, spec, spec), out_specs=spec, check_vma=False
        )(fade_rate, update_in, gate_in)

    return step
```

time: 19.8 us -> 19.4 us (0.980)
  Pallas kernels: 18.9 us -> 18.5 us
    pallas_call x1, Pallas kernels: 18.9 us -> 18.5 us  [local(): pl.pallas_call(functools.partial(kernel, outer, total_length), out_shape=...]
where the time goes in v3:
time: 19.4 us; the launch traced here: 19.3 us
  Pallas kernels  18.5 us (95%)
  local copies, waits for them, and re-layouts  0.8 us (4%)
    pallas_call x1, Pallas kernels, local(): pl.pallas_call(functools.partial(kernel, outer, total_length), out_shape=...  18.5 us
    unnamed x1, local copies, waits for them, and re-layouts  0.8 us

profile of v3, /device:TPU:1, one launch (start us, length us, event | category | flops | bytes accessed | tf_op | source)
XLA Modules:
  0.0 19.3 jit_solution(13798939251805107698)
XLA Ops:
  0.0 18.5 %shard_map.37 = bf16[2,512,256]{2,1,0:T(8,128)(2,1)S(1)} custom-call(f32[2,512,256]{2,1,0:T(8,128)} %fade_h.1, bf16[2,512,256]{2,1,0:T(8,128)(2,1)} %upd_h.1, bf16[2,512,256]{2,1,0:T(8,128)(2,1)} %gate_h.1), custom_call_target="tpu_custom_call" | custom-call | tf_op jit(solution)/shard_map/pallas_call | solution.py:270
  18.5 0.8 %copy.5 = bf16[2,512,256]{2,1,0:T(8,128)(2,1)} copy(bf16[2,512,256]{2,1,0:T(8,128)(2,1)S(1)} %shard_map.37) | data formatting | bytes 1048576

commit v4 on v3

--- a/solution.py
+++ b/solution.py
@@ -41,8 +41,8 @@
     outer, total_length,
     fade_h, upd_h, gate_h, out_ref,
     fade_v, upd_v, gate_v, lower, upper, logs, base, qv, rv, into,
-    row_out, row_in, far_out, far_in,
-    load_sem, gate_sem, row_send, row_recv, far_send, far_recv, told,
+    row_out, row_in, last_out, last_in, far_out, far_in,
+    load_sem, gate_sem, row_send, row_recv, last_send, last_recv, far_send, far_recv, told,
 ):
     batch, length, width = upd_v.shape
     parts = length // ROWS
@@ -97,41 +97,37 @@
     scale = math.log2(math.e) / total_length
     partner = at(z, r + 1 - 2 * core)
 
-    totals = {}
+    totals, entering = {}, {}
 
     def summary(b):
-        ups, downs = [], []
+        downs = []
         for p in range(parts):
             cut = (b, slice(p * ROWS, (p + 1) * ROWS))
             fade = fade_v[b * length + p * ROWS : b * length + (p + 1) * ROWS] * scale
             log = dot(lower[...], fade.astype(jnp.bfloat16))
             logs[cut] = log
-            push = upd_v[cut].astype(jnp.float32)
-            ups.append(folded(jnp.exp2(log) * push))
-            downs.append(folded(jnp.exp2(fade - log) * push))
+            downs.append(folded(jnp.exp2(fade - log) * upd_v[cut].astype(jnp.float32)))
             totals[b, p] = jnp.sum(folded(fade), axis=0, keepdims=True)
-        keeps = [jnp.exp2(-totals[b, p]) for p in range(parts)]
-        state = jnp.zeros((SUB, width), jnp.float32)
-        for p in range(parts):
-            into[0, b, p] = state
-            state = keeps[p] * (state + ups[p])
-        forward = jnp.sum(state, axis=0, keepdims=True)
         state = jnp.zeros((SUB, width), jnp.float32)
         for p in reversed(range(parts)):
-            into[1, b, p] = keeps[p] * state
-            state = downs[p] + keeps[p] * state
+            entering[b, p] = jnp.exp2(-totals[b, p]) * state
+            state = downs[p] + entering[b, p]
+            into[b, p] = entering[b, p]
         backward = jnp.sum(state, axis=0, keepdims=True)
         keep = jnp.exp2(-sum(totals[b, p] for p in range(parts)))
-        for k, value in enumerate((keep, forward, backward)):
+        for k, value in enumerate((keep, backward)):
             for t in range(tiles):
                 i = k * tiles + t
                 row_out[b, i : i + 1, :] = value[:, t * LANES : (t + 1) * LANES]
 
-    def send_row(b):
+    def send_row(src, dst, out_sem, in_sem):
         own = (1 - core) * CHIPS + x
         for k in others(own, INNER):
             place = k % CHIPS * CORES + 1 - k // CHIPS
-            send(row_out.at[b], row_in.at[b, r], row_send.at[b], row_recv.at[b], at(z, place))
+            send(src, dst.at[r], out_sem, in_sem, at(z, place))
+
+    def send_backward(b):
+        send_row(row_out.at[b], row_in.at[b], row_send.at[b], row_recv.at[b])
 
     loaded(0)
     summary(0)
@@ -145,24 +141,29 @@
     def _():
         pl.semaphore_wait(told, 1)
 
-    send_row(0)
+    send_backward(0)
     for b in range(1, batch):
         loaded(b)
         if b == batch - 1:
             pltpu.make_async_copy(gate_h, gate_v, gate_sem).start()
         summary(b)
-        send_row(b)
+        send_backward(b)
 
     upper[...] = triangle(ROWS, True)
 
     for b in range(batch):
+        state = jnp.zeros((1, width), jnp.float32)
         for p in range(parts):
             cut = (b, slice(p * ROWS, (p + 1) * ROWS))
             log = logs[cut]
             push = upd_v[cut].astype(jnp.float32)
-            enter = jnp.sum(into[0, b, p], axis=0, keepdims=True)
-            run = running(lower[...], jnp.exp2(log) * push) + enter
+            run = running(lower[...], jnp.exp2(log) * push) + state
+            state = run[ROWS - 1 :] * jnp.exp2(-totals[b, p])
             base[cut] = run * jnp.exp2(-log)
+        for t in range(tiles):
+            i = b * tiles + t
+            last_out[i : i + 1, :] = state[:, t * LANES : (t + 1) * LANES]
+    send_row(last_out, last_in, last_send, last_recv)
 
     @pl.when(core == 0)
     def _():
@@ -175,67 +176,76 @@
 
     zero, one = jnp.zeros((tiles, LANES), jnp.float32), jnp.ones((tiles, LANES), jnp.float32)
 
-    def combine_row(b):
+    def send_far(b, way, row):
+        for c in (1, 0):
+            send(
+                far_out.at[b, way], far_in.at[b, z], far_send, far_recv.at[b],
+                at(row, x * CORES + c),
+            )
+
+    before, after = {}, {}
+    for b in range(batch):
         row_in[b, pl.ds(r, 1)] = row_out[b][None]
         wait(row_in.at[b, pl.ds(0, INNER - 1)], row_recv.at[b])
         shares = [row_in[b, k] for k in range(INNER)]
-        shares = [(s[:tiles], s[tiles : 2 * tiles], s[2 * tiles :]) for s in shares]
-        keep_row, forward_row, backward_row = one, zero, zero
-        keep_before, forward_before = one, zero
+        keep_row, backward_row, keep_after, backward_after = one, zero, one, zero
+        for k in reversed(range(INNER)):
+            backward_row = shares[k][:tiles] * backward_row + shares[k][tiles:]
+            keep_row = shares[k][:tiles] * keep_row
+            keep_after = jnp.where(k > r, keep_row, keep_after)
+            backward_after = jnp.where(k > r, backward_row, backward_after)
+        after[b] = keep_after, backward_after
+        far_out[b, 0, :tiles] = keep_row
+        far_out[b, 1, :tiles] = keep_row
+        far_out[b, 1, tiles:] = backward_row
+        for row in range(outer - 1):
+
+            @pl.when((core == 1) & (row < z))
+            def _():
+                send_far(b, 1, row)
+
+    last_in[pl.ds(r, 1)] = last_out[...][None]
+    wait(last_in.at[pl.ds(0, INNER - 1)], last_recv)
+    for b in range(batch):
+        keep_row, forward_row, keep_before, forward_before = one, zero, one, zero
         for k in range(INNER):
-            keep, forward, _ = shares[k]
-            forward_row = keep * forward_row + forward
+            keep = row_in[b, k, :tiles]
+            forward_row = keep * forward_row + last_in[k, b * tiles : (b + 1) * tiles]
             keep_row = keep * keep_row
             keep_before = jnp.where(k < r, keep_row, keep_before)
             forward_before = jnp.where(k < r, forward_row, forward_before)
-        keep_part, keep_after, backward_after = one, one, zero
-        for k in reversed(range(INNER)):
-            keep, _, backward = shares[k]
-            backward_row = keep * backward_row + backward
-            keep_part = keep * keep_part
-            keep_after = jnp.where(k > r, keep_part, keep_after)
-            backward_after = jnp.where(k > r, backward_row, backward_after)
-        for k, last in enumerate((forward_row, backward_row)):
-            far_out[b, k, :tiles] = keep_row
-            far_out[b, k, tiles:] = last
-
-        @pl.when(core == 1)
-        def _():
-            for row in others(z, outer):
-                way = jnp.where(row > z, 0, 1)
-                for c in (1, 0):
-                    send(
-                        far_out.at[b, way], far_in.at[b, z], far_send, far_recv.at[b],
-                        at(row, x * CORES + c),
-                    )
-
-        return keep_before, forward_before, keep_after, backward_after
-
-    inside = [combine_row(b) for b in range(batch)]
+        before[b] = keep_before, forward_before
+        far_out[b, 0, tiles:] = forward_row
+        for row in range(1, outer):
+
+            @pl.when((core == 1) & (row > z))
+            def _():
+                send_far(b, 0, row)
 
     wait(gate_v, gate_sem)
     for b in range(batch):
-        before = jnp.zeros((1, width), jnp.float32)
+        passed = jnp.zeros((1, width), jnp.float32)
         for p in range(parts):
             cut = (b, slice(p * ROWS, (p + 1) * ROWS))
             log = logs[cut]
             short = log - fade_v[b * length + p * ROWS : b * length + (p + 1) * ROWS] * scale
             push = upd_v[cut].astype(jnp.float32)
-            enter = jnp.sum(into[1, b, p], axis=0, keepdims=True)
+            enter = jnp.sum(into[b, p], axis=0, keepdims=True)
             run = running(upper[...], jnp.exp2(-short) * push) + enter
             gate = gate_v[cut].astype(jnp.float32)
             gate = gate * (total_length**-0.5) / (1.0 + jnp.exp(-gate))
             raised = jnp.exp2(short) * gate
             base[cut] = base[cut] * gate + run * raised
-            after = sum(totals[b, q] for q in range(p, parts))
-            qv[cut] = jnp.exp2(-log) * gate * jnp.exp2(-before)
-            rv[cut] = raised * jnp.exp2(-after)
-            before = before + totals[b, p]
+            left = sum(totals[b, q] for q in range(p, parts))
+            qv[cut] = jnp.exp2(-log) * gate * jnp.exp2(-passed)
+            rv[cut] = raised * jnp.exp2(-left)
+            passed = passed + totals[b, p]
 
     for b in range(batch):
         far_in[b, pl.ds(z, 1)] = far_out[b, 0:1]
         wait(far_in.at[b, pl.ds(0, outer - 1)], far_recv.at[b])
-        keep_before, forward_before, keep_after, backward_after = inside[b]
+        keep_before, forward_before = before[b]
+        keep_after, backward_after = after[b]
         shares = [far_in[b, k] for k in range(outer)]
         enter_forward, enter_backward = zero, zero
         for k in range(outer):
@@ -255,6 +265,7 @@
 
     for b in range(batch):
         wait(row_in.at[b, pl.ds(0, INNER - 1)], row_send.at[b])
+    wait(last_in.at[pl.ds(0, INNER - 1)], last_send)
 
     @pl.when(core == 1)
     def _():
@@ -282,15 +293,19 @@
             pltpu.VMEM(full, f32),
             pltpu.VMEM(full, f32),
             pltpu.VMEM(full, f32),
-            pltpu.VMEM((2, batch, length // ROWS, SUB, width), f32),
-            pltpu.VMEM((batch, 3 * tiles, LANES), f32),
-            pltpu.VMEM((batch, INNER, 3 * tiles, LANES), f32),
+            pltpu.VMEM((batch, length // ROWS, SUB, width), f32),
+            pltpu.VMEM((batch, 2 * tiles, LANES), f32),
+            pltpu.VMEM((batch, INNER, 2 * tiles, LANES), f32),
+            pltpu.VMEM((batch * tiles, LANES), f32),
+            pltpu.VMEM((INNER, batch * tiles, LANES), f32),
             pltpu.VMEM((batch, 2, 2 * tiles, LANES), f32),
             pltpu.VMEM((batch, outer, 2 * tiles, LANES), f32),
             pltpu.SemaphoreType.DMA((batch,)),
             pltpu.SemaphoreType.DMA,
             pltpu.SemaphoreType.DMA((batch,)),
             pltpu.SemaphoreType.DMA((batch,)),
+            pltpu.SemaphoreType.DMA,
+            pltpu.SemaphoreType.DMA,
             pltpu.SemaphoreType.DMA,
             pltpu.SemaphoreType.DMA((batch,)),
             pltpu.SemaphoreType.REGULAR,

time: 19.4 us -> 19.2 us (0.990)
  Pallas kernels: 18.5 us -> 18.3 us
where the time goes in v4:
time: 19.2 us; the launch traced here: 19.1 us
  Pallas kernels  18.3 us (95%)
  local copies, waits for them, and re-layouts  0.8 us (4%)
    pallas_call x1, Pallas kernels, local(): pl.pallas_call(functools.partial(kernel, outer, total_length), out_shape=...  18.3 us
    unnamed x1, local copies, waits for them, and re-layouts  0.8 us

profile of v4, /device:TPU:1, one launch (start us, length us, event | category | flops | bytes accessed | tf_op | source)
XLA Modules:
  0.0 19.1 jit_solution(10822198263748747975)
XLA Ops:
  0.0 18.3 %shard_map.37 = bf16[2,512,256]{2,1,0:T(8,128)(2,1)S(1)} custom-call(f32[2,512,256]{2,1,0:T(8,128)} %fade_h.1, bf16[2,512,256]{2,1,0:T(8,128)(2,1)} %upd_h.1, bf16[2,512,256]{2,1,0:T(8,128)(2,1)} %gate_h.1), custom_call_target="tpu_custom_call" | custom-call | tf_op jit(solution)/shard_map/pallas_call | solution.py:281
  18.3 0.8 %copy.5 = bf16[2,512,256]{2,1,0:T(8,128)(2,1)} copy(bf16[2,512,256]{2,1,0:T(8,128)(2,1)S(1)} %shard_map.37) | data formatting | bytes 1048576

commit v5 on v4

--- a/solution.py
+++ b/solution.py
@@ -15,6 +15,7 @@
 LANES = 128
 ROWS = 128
 SUB = 8
+CUTS = 4
 
 
 def triangle(rows, upper):
@@ -39,10 +40,10 @@
 
 def kernel(
     outer, total_length,
-    fade_h, upd_h, gate_h, out_ref,
-    fade_v, upd_v, gate_v, lower, upper, logs, base, qv, rv, into,
-    row_out, row_in, last_out, last_in, far_out, far_in,
-    load_sem, gate_sem, row_send, row_recv, last_send, last_recv, far_send, far_recv, told,
+    fade_h, upd_h, gate_h, base, qv, rv, carried,
+    fade_v, upd_v, gate_v, lower, upper, logs, into,
+    row_out, row_in, last_out, last_in, far_out, far_in, as_sent,
+    load_sem, row_recv, last_recv, far_recv, sent, far_sent, told,
 ):
     batch, length, width = upd_v.shape
     parts = length // ROWS
@@ -103,11 +104,11 @@
         downs = []
         for p in range(parts):
             cut = (b, slice(p * ROWS, (p + 1) * ROWS))
-            fade = fade_v[b * length + p * ROWS : b * length + (p + 1) * ROWS] * scale
+            fade = fade_v[b * length + p * ROWS : b * length + (p + 1) * ROWS]
             log = dot(lower[...], fade.astype(jnp.bfloat16))
             logs[cut] = log
-            downs.append(folded(jnp.exp2(fade - log) * upd_v[cut].astype(jnp.float32)))
-            totals[b, p] = jnp.sum(folded(fade), axis=0, keepdims=True)
+            downs.append(folded(jnp.exp2((fade - log) * scale) * upd_v[cut].astype(jnp.float32)))
+            totals[b, p] = jnp.sum(folded(fade), axis=0, keepdims=True) * scale
         state = jnp.zeros((SUB, width), jnp.float32)
         for p in reversed(range(parts)):
             entering[b, p] = jnp.exp2(-totals[b, p]) * state
@@ -127,7 +128,7 @@
             send(src, dst.at[r], out_sem, in_sem, at(z, place))
 
     def send_backward(b):
-        send_row(row_out.at[b], row_in.at[b], row_send.at[b], row_recv.at[b])
+        send_row(row_out.at[b], row_in.at[b], sent, row_recv.at[b])
 
     loaded(0)
     summary(0)
@@ -144,18 +145,18 @@
     send_backward(0)
     for b in range(1, batch):
         loaded(b)
-        if b == batch - 1:
-            pltpu.make_async_copy(gate_h, gate_v, gate_sem).start()
         summary(b)
         send_backward(b)
 
+    load_gate = pltpu.make_async_copy(gate_h, gate_v, load_sem.at[0])
+    load_gate.start()
     upper[...] = triangle(ROWS, True)
 
     for b in range(batch):
         state = jnp.zeros((1, width), jnp.float32)
         for p in range(parts):
             cut = (b, slice(p * ROWS, (p + 1) * ROWS))
-            log = logs[cut]
+            log = logs[cut] * scale
             push = upd_v[cut].astype(jnp.float32)
             run = running(lower[...], jnp.exp2(log) * push) + state
             state = run[ROWS - 1 :] * jnp.exp2(-totals[b, p])
@@ -163,7 +164,7 @@
         for t in range(tiles):
             i = b * tiles + t
             last_out[i : i + 1, :] = state[:, t * LANES : (t + 1) * LANES]
-    send_row(last_out, last_in, last_send, last_recv)
+    send_row(last_out, last_in, sent, last_recv)
 
     @pl.when(core == 0)
     def _():
@@ -179,7 +180,7 @@
     def send_far(b, way, row):
         for c in (1, 0):
             send(
-                far_out.at[b, way], far_in.at[b, z], far_send, far_recv.at[b],
+                far_out.at[b, way], far_in.at[b, z], far_sent, far_recv.at[b],
                 at(row, x * CORES + c),
             )
 
@@ -222,12 +223,12 @@
             def _():
                 send_far(b, 0, row)
 
-    wait(gate_v, gate_sem)
+    load_gate.wait()
     for b in range(batch):
         passed = jnp.zeros((1, width), jnp.float32)
         for p in range(parts):
             cut = (b, slice(p * ROWS, (p + 1) * ROWS))
-            log = logs[cut]
+            log = logs[cut] * scale
             short = log - fade_v[b * length + p * ROWS : b * length + (p + 1) * ROWS] * scale
             push = upd_v[cut].astype(jnp.float32)
             enter = jnp.sum(into[b, p], axis=0, keepdims=True)
@@ -258,19 +259,40 @@
         enter_backward = keep_after * enter_backward + backward_after
         for t in range(tiles):
             cut = slice(t * LANES, (t + 1) * LANES)
-            ahead, behind = enter_forward[t : t + 1], enter_backward[t : t + 1]
-            out_ref[b, :, cut] = (
-                base[b, :, cut] + qv[b, :, cut] * ahead + rv[b, :, cut] * behind
-            ).astype(out_ref.dtype)
-
-    for b in range(batch):
-        wait(row_in.at[b, pl.ds(0, INNER - 1)], row_send.at[b])
-    wait(last_in.at[pl.ds(0, INNER - 1)], last_send)
+            carried[0, b, :, cut] = enter_forward[t : t + 1]
+            carried[1, b, :, cut] = enter_backward[t : t + 1]
+
+    line = width // LANES
+    wait(as_sent, sent)
 
     @pl.when(core == 1)
     def _():
-        sent = batch * CORES * (outer - 1) * 2 * tiles * LANES // width
-        wait(fade_v.at[pl.ds(0, sent)], far_send)
+        wait(fade_v.at[pl.ds(0, 2 * batch * tiles * CORES * (outer - 1) // line)], far_sent)
+
+
+def finish_kernel(base, ahead, behind, enter, out_h, out_v, sem):
+    batch, length, _ = base.shape
+    copies = []
+    for b in range(batch):
+        for c in range(CUTS):
+            cut = (b, pl.ds(c * (length // CUTS), length // CUTS))
+            out_v[cut] = (
+                base[cut] + ahead[cut] * enter[0, b] + behind[cut] * enter[1, b]
+            ).astype(out_v.dtype)
+            copies.append(pltpu.make_async_copy(out_v.at[cut], out_h.at[cut], sem))
+            copies[-1].start()
+    pltpu.make_async_copy(out_v, out_h, sem).wait()
+
+
+def finish(base, ahead, behind, enter, kind):
+    return pl.pallas_call(
+        finish_kernel,
+        out_shape=jax.ShapeDtypeStruct(base.shape, kind),
+        in_specs=[pl.BlockSpec(memory_space=pltpu.VMEM)] * 4,
+        out_specs=pl.BlockSpec(memory_space=pltpu.HBM),
+        scratch_shapes=[pltpu.VMEM(base.shape, kind), pltpu.SemaphoreType.DMA],
+        compiler_params=pltpu.CompilerParams(vmem_limit_bytes=8 * 2**20),
+    )(base, ahead, behind, enter)
 
 
 def local(outer, total_length, fade_rate, update_in, gate_in):
@@ -278,20 +300,18 @@
     tiles = width // LANES
     full, f32 = (batch, length, width), jnp.float32
     arguments = (fade_rate, update_in, gate_in)
-    return pl.pallas_call(
+    base, ahead, behind, enter = pl.pallas_call(
         functools.partial(kernel, outer, total_length),
-        out_shape=jax.ShapeDtypeStruct(full, update_in.dtype),
+        out_shape=[jax.ShapeDtypeStruct(full, f32)] * 3
+        + [jax.ShapeDtypeStruct((2, batch, 1, width), f32)],
         in_specs=[pl.BlockSpec(memory_space=pltpu.HBM)] * 3,
-        out_specs=pl.BlockSpec(memory_space=pltpu.VMEM),
+        out_specs=[pl.BlockSpec(memory_space=pltpu.VMEM)] * 4,
         scratch_shapes=[
             pltpu.VMEM((batch * length, width), f32),
             pltpu.VMEM(full, update_in.dtype),
             pltpu.VMEM(full, gate_in.dtype),
             pltpu.VMEM((ROWS, ROWS), jnp.bfloat16),
             pltpu.VMEM((ROWS, ROWS), jnp.bfloat16),
-            pltpu.VMEM(full, f32),
-            pltpu.VMEM(full, f32),
-            pltpu.VMEM(full, f32),
             pltpu.VMEM(full, f32),
             pltpu.VMEM((batch, length // ROWS, SUB, width), f32),
             pltpu.VMEM((batch, 2 * tiles, LANES), f32),
@@ -300,20 +320,20 @@
             pltpu.VMEM((INNER, batch * tiles, LANES), f32),
             pltpu.VMEM((batch, 2, 2 * tiles, LANES), f32),
             pltpu.VMEM((batch, outer, 2 * tiles, LANES), f32),
+            pltpu.VMEM((INNER - 1, 3 * batch, tiles, LANES), f32),
+            pltpu.SemaphoreType.DMA((batch,)),
             pltpu.SemaphoreType.DMA((batch,)),
             pltpu.SemaphoreType.DMA,
             pltpu.SemaphoreType.DMA((batch,)),
-            pltpu.SemaphoreType.DMA((batch,)),
             pltpu.SemaphoreType.DMA,
             pltpu.SemaphoreType.DMA,
-            pltpu.SemaphoreType.DMA,
-            pltpu.SemaphoreType.DMA((batch,)),
             pltpu.SemaphoreType.REGULAR,
         ],
         compiler_params=pltpu.CompilerParams(
             collective_id=0, has_side_effects=True, vmem_limit_bytes=32 * 2**20
         ),
     )(*(pltpu.with_memory_space_constraint(a, pltpu.HBM) for a in arguments))
+    return finish(base, ahead, behind, enter, update_in.dtype)
 
 
 def solution(mesh):

time: 19.2 us -> 19.1 us (level)
  local copies, waits for them, and re-layouts: 0.8 us -> 0 us
  Pallas kernels: 18.3 us -> 19 us
    pallas_call x0 -> x1, Pallas kernels: none -> 0.81 us  [finish(): pl.pallas_call(finish_kernel, out_shape=jax.ShapeDtypeStruct(base.shape,...]
    unnamed x1 -> x0, local copies, waits for them, and re-layouts: 0.8 us -> none
where the time goes in v5:
time: 19.1 us; the launch traced here: 19 us
  Pallas kernels  19 us (99%)
    pallas_call x1, Pallas kernels, local(): pl.pallas_call(functools.partial(kernel, outer, total_length), out_shape=...  18.2 us
    pallas_call x1, Pallas kernels, finish(): pl.pallas_call(finish_kernel, out_shape=jax.ShapeDtypeStruct(base.shape,...  0.81 us

profile of v5, /device:TPU:1, one launch (start us, length us, event | category | flops | bytes accessed | tf_op | source)
XLA Modules:
  0.0 19.0 jit_solution(5208975406895234354)
XLA Ops:
  0.0 18.2 %shard_map.37 = (f32[2,512,256]{2,1,0:T(8,128)S(1)}, f32[2,512,256]{2,1,0:T(8,128)S(1)}, f32[2,512,256]{2,1,0:T(8,128)S(1)}, f32[2,2,1,256]{3,2,1,0:T(1,128)S(1)}) custom-call(f32[2,512,256]{2,1,0:T(8,128)} %fade_h.1, bf16[2,512,256]{2,1,0:T(8,128)(2,1)} %upd_h.1, bf16[2,512,256]{2,1,0:T(8,128)(2,1)} %gate_h.1), custom_call_target="tpu_custom_call" | custom-call | tf_op jit(solution)/shard_map/pallas_call | solution.py:303
  18.2 0.8 %shard_map.38 = bf16[2,512,256]{2,1,0:T(8,128)(2,1)} custom-call(f32[2,512,256]{2,1,0:T(8,128)S(1)} %get-tuple-element.9.base, f32[2,512,256]{2,1,0:T(8,128)S(1)} %get-tuple-element.10.ahead, f32[2,512,256]{2,1,0:T(8,128)S(1)} %get-tuple-element.11.behind, f32[2,2,1,256]{3,2,1,0:T(1,128)S(1)} %get-tuple-element.12.enter), custom_call_target="tpu_custom_call" | custom-call | tf_op jit(solution)/shard_map/pallas_call | solution.py:288

commit v6 on v5

--- a/solution.py
+++ b/solution.py
@@ -104,11 +104,11 @@
         downs = []
         for p in range(parts):
             cut = (b, slice(p * ROWS, (p + 1) * ROWS))
-            fade = fade_v[b * length + p * ROWS : b * length + (p + 1) * ROWS]
+            fade = fade_v[b * length + p * ROWS : b * length + (p + 1) * ROWS] * scale
             log = dot(lower[...], fade.astype(jnp.bfloat16))
             logs[cut] = log
-            downs.append(folded(jnp.exp2((fade - log) * scale) * upd_v[cut].astype(jnp.float32)))
-            totals[b, p] = jnp.sum(folded(fade), axis=0, keepdims=True) * scale
+            downs.append(folded(jnp.exp2(fade - log) * upd_v[cut].astype(jnp.float32)))
+            totals[b, p] = jnp.sum(folded(fade), axis=0, keepdims=True)
         state = jnp.zeros((SUB, width), jnp.float32)
         for p in reversed(range(parts)):
             entering[b, p] = jnp.exp2(-totals[b, p]) * state
@@ -156,7 +156,7 @@
         state = jnp.zeros((1, width), jnp.float32)
         for p in range(parts):
             cut = (b, slice(p * ROWS, (p + 1) * ROWS))
-            log = logs[cut] * scale
+            log = logs[cut]
             push = upd_v[cut].astype(jnp.float32)
             run = running(lower[...], jnp.exp2(log) * push) + state
             state = run[ROWS - 1 :] * jnp.exp2(-totals[b, p])
@@ -228,7 +228,7 @@
         passed = jnp.zeros((1, width), jnp.float32)
         for p in range(parts):
             cut = (b, slice(p * ROWS, (p + 1) * ROWS))
-            log = logs[cut] * scale
+            log = logs[cut]
             short = log - fade_v[b * length + p * ROWS : b * length + (p + 1) * ROWS] * scale
             push = upd_v[cut].astype(jnp.float32)
             enter = jnp.sum(into[b, p], axis=0, keepdims=True)

time: 19.1 us -> 19.1 us (level)
  no operation moved by 1% of the time
where the time goes in v6:
time: 19.1 us; the launch traced here: 19 us
  Pallas kernels  19 us (99%)
    pallas_call x1, Pallas kernels, local(): pl.pallas_call(functools.partial(kernel, outer, total_length), out_shape=...  18.2 us
    pallas_call x1, Pallas kernels, finish(): pl.pallas_call(finish_kernel, out_shape=jax.ShapeDtypeStruct(base.shape,...  0.81 us

profile of v6, /device:TPU:1, one launch (start us, length us, event | category | flops | bytes accessed | tf_op | source)
XLA Modules:
  0.0 19.0 jit_solution(5868804903720530510)
XLA Ops:
  0.0 18.2 %shard_map.37 = (f32[2,512,256]{2,1,0:T(8,128)S(1)}, f32[2,512,256]{2,1,0:T(8,128)S(1)}, f32[2,512,256]{2,1,0:T(8,128)S(1)}, f32[2,2,1,256]{3,2,1,0:T(1,128)S(1)}) custom-call(f32[2,512,256]{2,1,0:T(8,128)} %fade_h.1, bf16[2,512,256]{2,1,0:T(8,128)(2,1)} %upd_h.1, bf16[2,512,256]{2,1,0:T(8,128)(2,1)} %gate_h.1), custom_call_target="tpu_custom_call" | custom-call | tf_op jit(solution)/shard_map/pallas_call | solution.py:303
  18.2 0.8 %shard_map.38 = bf16[2,512,256]{2,1,0:T(8,128)(2,1)} custom-call(f32[2,512,256]{2,1,0:T(8,128)S(1)} %get-tuple-element.9.base, f32[2,512,256]{2,1,0:T(8,128)S(1)} %get-tuple-element.10.ahead, f32[2,512,256]{2,1,0:T(8,128)S(1)} %get-tuple-element.11.behind, f32[2,2,1,256]{3,2,1,0:T(1,128)S(1)} %get-tuple-element.12.enter), custom_call_target="tpu_custom_call" | custom-call | tf_op jit(solution)/shard_map/pallas_call | solution.py:288

commit v7 on v6

--- a/solution.py
+++ b/solution.py
@@ -36,6 +36,13 @@
 
 def folded(value):
     return jnp.sum(value.reshape(value.shape[0] // SUB, SUB, value.shape[1]), axis=0)
+
+
+def joined(pairs):
+    while len(pairs) > 1:
+        ends = [(p[0] * q[0], p[1] + p[0] * q[1]) for p, q in zip(pairs[::2], pairs[1::2])]
+        pairs = ends + pairs[len(pairs) // 2 * 2 :]
+    return pairs[0][1]
 
 
 def kernel(
@@ -247,14 +254,13 @@
         wait(far_in.at[b, pl.ds(0, outer - 1)], far_recv.at[b])
         keep_before, forward_before = before[b]
         keep_after, backward_after = after[b]
-        shares = [far_in[b, k] for k in range(outer)]
-        enter_forward, enter_backward = zero, zero
-        for k in range(outer):
-            new = shares[k][:tiles] * enter_forward + shares[k][tiles:]
-            enter_forward = jnp.where(k < z, new, enter_forward)
-        for k in reversed(range(outer)):
-            new = shares[k][:tiles] * enter_backward + shares[k][tiles:]
-            enter_backward = jnp.where(k > z, new, enter_backward)
+        shares = [(far_in[b, k, :tiles], far_in[b, k, tiles:]) for k in range(outer)]
+
+        def taken(k, wanted):
+            return tuple(jnp.where(wanted, v, e) for v, e in zip(shares[k], (one, zero)))
+
+        enter_forward = joined([taken(k, k < z) for k in reversed(range(outer))])
+        enter_backward = joined([taken(k, k > z) for k in range(outer)])
         enter_forward = keep_before * enter_forward + forward_before
         enter_backward = keep_after * enter_backward + backward_after
         for t in range(tiles):

time: 19.1 us -> 19.1 us (level)
  no operation moved by 1% of the time
where the time goes in v7:
time: 19.1 us; the launch traced here: 19 us
  Pallas kernels  19 us (99%)
    pallas_call x1, Pallas kernels, local(): pl.pallas_call(functools.partial(kernel, outer, total_length), out_shape=...  18.2 us
    pallas_call x1, Pallas kernels, finish(): pl.pallas_call(finish_kernel, out_shape=jax.ShapeDtypeStruct(base.shape,...  0.81 us

profile of v7, /device:TPU:1, one launch (start us, length us, event | category | flops | bytes accessed | tf_op | source)
XLA Modules:
  0.0 19.0 jit_solution(3333652434779171570)
XLA Ops:
  0.0 18.2 %shard_map.37 = (f32[2,512,256]{2,1,0:T(8,128)S(1)}, f32[2,512,256]{2,1,0:T(8,128)S(1)}, f32[2,512,256]{2,1,0:T(8,128)S(1)}, f32[2,2,1,256]{3,2,1,0:T(1,128)S(1)}) custom-call(f32[2,512,256]{2,1,0:T(8,128)} %fade_h.1, bf16[2,512,256]{2,1,0:T(8,128)(2,1)} %upd_h.1, bf16[2,512,256]{2,1,0:T(8,128)(2,1)} %gate_h.1), custom_call_target="tpu_custom_call" | custom-call | tf_op jit(solution)/shard_map/pallas_call | solution.py:309
  18.2 0.8 %shard_map.38 = bf16[2,512,256]{2,1,0:T(8,128)(2,1)} custom-call(f32[2,512,256]{2,1,0:T(8,128)S(1)} %get-tuple-element.9.base, f32[2,512,256]{2,1,0:T(8,128)S(1)} %get-tuple-element.10.ahead, f32[2,512,256]{2,1,0:T(8,128)S(1)} %get-tuple-element.11.behind, f32[2,2,1,256]{3,2,1,0:T(1,128)S(1)} %get-tuple-element.12.enter), custom_call_target="tpu_custom_call" | custom-call | tf_op jit(solution)/shard_map/pallas_call | solution.py:294
